TPU v7x, 32 devices: a whole 2x2x4 slice. The times are simulated.
32 devices in a mesh: px: 2 (over core), pz: 16 (over z, y, x).
Axes of the slice: x: 2, y: 2, z: 4, core: 2. Of those that a mesh axis runs over, the one named last changes fastest.
Arguments:
- velocity: float32 [3, 256, 32, 256], P(None, 'pz', None, 'px'), may hold values from -8 to 8, as said below
- filter_inverse: float32 [256, 256], replicated, may hold values from 0 to 2, as said below
- filter_block: int32 [256], replicated, may hold values from 0 to 7, never falling along the last dimension, each value on 1 to 128 neighbouring positions
- plane_bin: int32 [256], replicated, may hold values from 0 to 63, never falling along the last dimension, each value on 1 to 16 neighbouring positions
Outputs:
- leonard: float32 [6, 256, 32, 256], P(None, 'pz', None, 'px')
- viscosity: float32 [256, 32, 256], P('pz', None, 'px')
- coefficient: float32 [256], replicated
Inputs may be any that keep to these rules, and one draw needn't show every extreme that they name: `velocity`: each component is a rough random field. `filter_inverse`: entries are positive. `filter_block`: never falls along the planes; each of the 8 blocks holds 1 to 128 consecutive planes, one exactly 128. `plane_bin`: never falls along the planes; each of the 64 bins holds 1 to 16 consecutive planes, one exactly 16.
All inputs are finite; a program needn't handle non-finite values.
Results may differ from a plain program's by a relative error of at most 0.0003.
Values sent between devices are 32-bit elements; how exact they have to be, the bound alone decides.
A program may use at most 128 MiB of HBM per device.

v0:
```python
import jax
import jax.numpy as jnp
from jax import lax
from jax.sharding import PartitionSpec as P

NBIN = 64


def with_halo(cells, sides, width, closed):
    for axis, dim in sides:
        count = lax.axis_size(axis)
        ends = count if closed else count - 1
        head = lax.slice_in_dim(cells, 0, width, axis=dim)
        tail = lax.slice_in_dim(cells, cells.shape[dim] - width, cells.shape[dim], axis=dim)
        cells = jnp.concatenate(
            [
                lax.ppermute(tail, axis, [(i, (i + 1) % count) for i in range(ends)]),
                cells,
                lax.ppermute(head, axis, [((i + 1) % count, i) for i in range(ends)]),
            ],
            axis=dim,
        )
    return cells


def quantities(padded):
    centre = padded[:, 1:-1, 1:-1, 1:-1]
    along_y = (padded[:, 2:, 1:-1, 1:-1] - padded[:, :-2, 1:-1, 1:-1]) * 0.5
    along_z = (padded[:, 1:-1, 2:, 1:-1] - padded[:, 1:-1, :-2, 1:-1]) * 0.5
    along_x = (padded[:, 1:-1, 1:-1, 2:] - padded[:, 1:-1, 1:-1, :-2]) * 0.5
    strain = jnp.stack(
        [
            along_x[0],
            along_y[1],
            along_z[2],
            0.5 * (along_y[0] + along_x[1]),
            0.5 * (along_z[0] + along_x[2]),
            0.5 * (along_z[1] + along_y[2]),
        ]
    )
    magnitude = jnp.sqrt(
        2.0 * jnp.sum(strain[:3] * strain[:3], axis=0)
        + 4.0 * jnp.sum(strain[3:] * strain[3:], axis=0)
    )
    products = jnp.stack(
        [
            centre[0] * centre[0],
            centre[1] * centre[1],
            centre[2] * centre[2],
            centre[0] * centre[1],
            centre[0] * centre[2],
            centre[1] * centre[2],
        ]
    )
    fields = jnp.concatenate([centre, strain, products, magnitude[None] * strain], axis=0)
    along = (fields[..., :-2] + 2.0 * fields[..., 1:-1] + fields[..., 2:]) * 0.25
    boxed = (along[:, :, :-2] + 2.0 * along[:, :, 1:-1] + along[:, :, 2:]) * 0.25
    return (boxed, magnitude[:, 1:-1, 1:-1])


def contract(filtered):
    speed = filtered[0:3]
    strain = filtered[3:9]
    products = filtered[9:15]
    scaled = filtered[15:21]
    leonard = products - jnp.stack(
        [
            speed[0] * speed[0],
            speed[1] * speed[1],
            speed[2] * speed[2],
            speed[0] * speed[1],
            speed[0] * speed[2],
            speed[1] * speed[2],
        ]
    )
    fmag = jnp.sqrt(
        2.0 * jnp.sum(strain[:3] * strain[:3], axis=0)
        + 4.0 * jnp.sum(strain[3:] * strain[3:], axis=0)
    )
    model = scaled - 4.0 * fmag[None] * strain
    weights = jnp.array([1.0, 1.0, 1.0, 2.0, 2.0, 2.0], jnp.float32).reshape(6, 1, 1, 1)
    product_lm = jnp.sum(weights * leonard * model, axis=0)
    product_mm = jnp.sum(weights * model * model, axis=0)
    return (leonard, product_lm, product_mm)


def local(velocity, filter_inverse, filter_block, plane_bin):
    same = (filter_block[:, None] == filter_block[None, :]).astype(jnp.float32)
    masked = filter_inverse * same
    weights = masked / jnp.sum(masked, axis=1, keepdims=True)
    local_planes = velocity.shape[1]
    extended = with_halo(velocity, (("px", 3),), 2, True)
    extended = with_halo(extended, (("pz", 1),), 1, False)
    extended = jnp.concatenate([extended[:, :, -2:], extended, extended[:, :, :2]], axis=2)
    boxed, magnitude = quantities(extended)
    smooth_boxed = lax.all_to_all(boxed, "pz", split_axis=2, concat_axis=1, tiled=True)
    filtered = jnp.einsum("ab,kbzx->kazx", weights, smooth_boxed, precision=lax.Precision.HIGHEST)
    leonard, product_lm, product_mm = contract(filtered)
    onehot = (plane_bin[:, None] == jnp.arange(NBIN, dtype=jnp.int32)[None, :]).astype(jnp.float32)
    local_lm = jnp.dot(jnp.sum(product_lm, axis=(1, 2)), onehot, precision=lax.Precision.HIGHEST)
    local_mm = jnp.dot(jnp.sum(product_mm, axis=(1, 2)), onehot, precision=lax.Precision.HIGHEST)
    numer, denom = lax.psum((local_lm, local_mm), ("px", "pz"))
    cells = filtered.shape[3] * lax.axis_size("px") * filtered.shape[2] * lax.axis_size("pz")
    per_bin = numer / jnp.maximum(denom, jnp.float32(cells))
    coefficient = jnp.dot(onehot, per_bin, precision=lax.Precision.HIGHEST)
    leonard_back = lax.all_to_all(leonard, "pz", split_axis=1, concat_axis=2, tiled=True)
    offset = lax.axis_index("pz") * local_planes
    local_coef = lax.dynamic_slice_in_dim(coefficient, offset, local_planes, 0)
    viscosity = local_coef[:, None, None] * magnitude
    return (leonard_back, viscosity, coefficient)


def solution(mesh):
    return jax.shard_map(
        local,
        mesh=mesh,
        in_specs=(P(None, "pz", None, "px"), P(), P(), P()),
        out_specs=(P(None, "pz", None, "px"), P("pz", None, "px"), P()),
        check_vma=False,
    )
```

profile of v0, /device:TPU:0, one launch (start us, length us, event | category | flops | bytes accessed | tf_op | source)
XLA Modules:
  0.0 246.9 jit_solution(18244381259723919933)
XLA Ops:
  0.6 1.7 fusion.38
  2.4 0.4 copy.41
  2.7 0.5 collective-permute-start
  3.3 0.3 copy.42
  3.7 0.5 copy.24
  4.2 0.4 copy.23
  4.9 0.4 copy.25
  5.3 0.7 pad_maximum_fusion.18
  6.0 4.6 %collective-permute-start.2 = (f32[3,1,32,132]{3,1,0,2:T(1,128)S(1)}, f32[3,1,32,132]{3,1,0,2:T(1,128)S(1)}, u32[]{:S(2)}, u32[]{:S(2)}) collective-permute-start(f32[3,1,32,132]{3,1,0,2:T(1,128)S(1)} %get-tuple-element.27), channel_id=1, source_target_pairs={{0,1},{1,2},{2,3},{3,4},{4,5},{5,6},{6,7},{7,8},{8,9},{9,10},{10,1... | collective-permute-start | bytes 152072 | tf_op jit(solution)/shard_map/ppermute | solution.py:17
  10.6 1.5 collective-permute-start.3
  12.1 1.0 collective-permute-done.2
  13.1 4.1 %collective-permute-done.3 = f32[3,1,32,132]{3,1,0,2:T(1,128)S(1)} collective-permute-done((f32[3,1,32,132]{3,1,0,2:T(1,128)S(1)}, f32[3,1,32,132]{3,1,0,2:T(1,128)S(1)}, u32[]{:S(2)}, u32[]{:S(2)}) %collective-permute-start.3) | collective-permute-done | bytes 50720 | tf_op jit(solution)/shard_map/ppermute | solution.py:19
  17.4 1.0 pad_maximum_fusion
  18.5 3.0 %fusion.6 = (f32[3,16,34,130]{3,1,0,2:T(8,128)}, f32[3,16,34,130]{3,1,0,2:T(8,128)S(1)}, f32[21,16,34,130]{3,1,0,2:T(8,128)S(1)}) fusion(f32[3,18,36,132]{3,1,0,2:T(8,128)S(1)} %pad_maximum_fusion), kind=kLoop, calls=%fused_computation.25 | loop fusion | flops 848639 | bytes 8434176 | tf_op jit(solution)/shard_map/mul | solution.py:28
  21.6 1.2 fusion.36
  22.8 2.1 fusion.5
  26.6 0.4 multiply_dynamic-update-slice_fusion.3
  26.9 0.4 multiply_dynamic-update-slice_fusion.2
  27.3 0.4 multiply_dynamic-update-slice_fusion.1
  28.1 0.5 multiply_dynamic-update-slice_fusion
  28.7 3.2 %fusion = f32[21,16,34,128]{3,1,0,2:T(8,128)S(1)} fusion(f32[21,16,34,130]{3,1,0,2:T(8,128)S(1)} %multiply_dynamic-update-slice_fusion), kind=kLoop, calls=%fused_computation.1 | loop fusion | flops 5849088 | bytes 23396352 | tf_op jit(solution)/shard_map/mul | solution.py:56
  31.9 3.2 %fusion.2 = f32[21,16,32,128]{3,1,0,2:T(8,128)} fusion(f32[21,16,34,128]{3,1,0,2:T(8,128)S(1)} %fusion), kind=kLoop, calls=%fused_computation.5 | loop fusion | flops 5505024 | bytes 22020096 | tf_op jit(solution)/shard_map/mul | solution.py:57
  35.0 7.8 %all-to-all-start = ((f32[21,16,32,128]{3,1,0,2:T(8,128)}), f32[21,16,32,128]{3,1,0,2:T(8,128)}, u32[]{:S(2)}, u32[]{:S(2)}) async-start(f32[21,16,32,128]{3,1,0,2:T(8,128)} %fusion.2), calls=%async_computation | async-start | bytes 11010048 | tf_op jit(solution)/shard_map/all_to_all | solution.py:96
  43.1 102.0 %all-to-all-done = f32[21,16,32,128]{3,1,0,2:T(8,128)} async-done(((f32[21,16,32,128]{3,1,0,2:T(8,128)}), f32[21,16,32,128]{3,1,0,2:T(8,128)}, u32[]{:S(2)}, u32[]{:S(2)}) %all-to-all-start) | async-done | bytes 5505056 | tf_op jit(solution)/shard_map/all_to_all | solution.py:96
  145.1 3.3 %copy.29 = f32[21,16,16,2,128]{4,2,1,3,0:T(8,128)S(1)} copy(f32[21,16,16,2,128]{4,2,0,3,1:T(8,128)} %bitcast.2) | data formatting | bytes 11010048 | tf_op jit(solution)/shard_map/all_to_all | solution.py:96
  148.4 8.8 %convolution_bitcast_fusion = f32[21,256,2,128]{1,3,2,0:T(8,128)S(1)} fusion(f32[21,256,2,128]{3,1,2,0:T(8,128)S(1)} %bitcast.28, f32[256,256]{1,0:T(8,128)S(1)} %copy-done.2, f32[256]{0:T(256)S(1)} %fusion.19, s32[256]{0:T(256)S(1)} %copy-done.3), kind=kOutput, calls=%fused_computation.10 | convolution fusion | flops 4228055040 | bytes 11274240 | tf_op jit(solution)/shard_map/ab,kbzx->kazx/dot_general | solution.py:97
  158.0 0.7 fusion.10
  158.7 2.1 copy.31
  160.8 25.5 %all-to-all-start.1 = ((f32[6,256,2,128]{3,2,0,1:T(2,128)}), f32[6,256,2,128]{3,2,0,1:T(2,128)S(1)}, u32[]{:S(2)}, u32[]{:S(2)}) async-start(f32[6,256,2,128]{3,2,0,1:T(2,128)} %copy.31), calls=%async_computation.1 | async-start | bytes 3145728 | tf_op jit(solution)/shard_map/all_to_all | solution.py:106
  186.8 56.8 %all-reduce = (f32[64]{0:T(128)S(1)}, f32[64]{0:T(128)S(1)}) all-reduce(f32[64]{0:T(128)S(1)} %convolution_bitcast_fusion.2, f32[64]{0:T(128)S(1)} %convolution_bitcast_fusion.1), channel_id=1, replica_groups=mesh['px'=2,'pz'=16] {'px','pz'}, use_global_device_ids=true, to_apply=%region_6.0 | all-reduce | flops 128 | bytes 1024 | tf_op jit(solution)/shard_map/psum | solution.py:102
  244.1 0.8 copy.35
  245.2 1.6 copy.34
  (48 shorter events, 4.8 us)
Async XLA Ops:
  0.6 3.1 %copy-start = (f32[3,16,32,128]{3,2,1,0:T(8,128)S(1)}, f32[3,16,32,128]{3,2,1,0:T(8,128)}, u32[]{:S(2)}) copy-start(f32[3,16,32,128]{3,2,1,0:T(8,128)} %param.5) | copy-start | bytes 2359300
  2.7 1.4 collective-permute-start
  3.6 1.3 collective-permute-start.1
  6.0 7.1 %collective-permute-start.2 = (f32[3,1,32,132]{3,1,0,2:T(1,128)S(1)}, f32[3,1,32,132]{3,1,0,2:T(1,128)S(1)}, u32[]{:S(2)}, u32[]{:S(2)}) collective-permute-start(f32[3,1,32,132]{3,1,0,2:T(1,128)S(1)} %get-tuple-element.27), channel_id=1, source_target_pairs={{0,1},{1,2},{2,3},{3,4},{4,5},{5,6},{6,7},{7,8},{8,9},{9,10},{10,1... | collective-permute-start | bytes 152072 | tf_op jit(solution)/shard_map/ppermute | solution.py:17
  10.6 6.6 %collective-permute-start.3 = (f32[3,1,32,132]{3,1,0,2:T(1,128)S(1)}, f32[3,1,32,132]{3,1,0,2:T(1,128)S(1)}, u32[]{:S(2)}, u32[]{:S(2)}) collective-permute-start(f32[3,1,32,132]{3,1,0,2:T(1,128)S(1)} %get-tuple-element.28), channel_id=1, source_target_pairs={{1,0},{2,1},{3,2},{4,3},{5,4},{6,5},{7,6},{8,7},{9,8},{10,9},{11,1... | collective-permute-start | bytes 152072 | tf_op jit(solution)/shard_map/ppermute | solution.py:19
  22.8 2.3 copy-start.1
  35.0 7.9 %copy-start.2 = (f32[256,256]{1,0:T(8,128)S(1)}, f32[256,256]{1,0:T(8,128)}, u32[]{:S(2)}) copy-start(f32[256,256]{1,0:T(8,128)} %param.6) | copy-start | bytes 786436
  35.0 7.9 %copy-start.3 = (s32[256]{0:T(256)S(1)}, s32[256]{0:T(256)}, u32[]{:S(2)}) copy-start(s32[256]{0:T(256)} %param.7) | copy-start | bytes 3076
  35.0 110.0 %all-to-all-start = ((f32[21,16,32,128]{3,1,0,2:T(8,128)}), f32[21,16,32,128]{3,1,0,2:T(8,128)}, u32[]{:S(2)}, u32[]{:S(2)}) async-start(f32[21,16,32,128]{3,1,0,2:T(8,128)} %fusion.2), calls=%async_computation | async-start | bytes 11010048 | tf_op jit(solution)/shard_map/all_to_all | solution.py:96
  157.3 0.7 copy-start.4
  158.7 27.6 %copy-start.5 = (s32[256]{0:T(256)S(1)}, s32[256]{0:T(256)}, u32[]{:S(2)}) copy-start(s32[256]{0:T(256)} %param.8) | copy-start | bytes 3076
  160.8 84.1 %all-to-all-start.1 = ((f32[6,256,2,128]{3,2,0,1:T(2,128)}), f32[6,256,2,128]{3,2,0,1:T(2,128)S(1)}, u32[]{:S(2)}, u32[]{:S(2)}) async-start(f32[6,256,2,128]{3,2,0,1:T(2,128)} %copy.31), calls=%async_computation.1 | async-start | bytes 3145728 | tf_op jit(solution)/shard_map/all_to_all | solution.py:106
  243.8 1.4 copy-start.6
where the time goes:
time: 247 us
  waiting for transfers between devices  107 us (43%)
  blocking collectives  56.8 us (23%)
  starting transfers between devices  40 us (16%)
  other arithmetic  18.2 us (7%)
  local copies, waits for them, and re-layouts  14 us (6%)
  matrix products  9.47 us (4%)
    all_to_all x1, waiting for transfers between devices, local(): lax.all_to_all(boxed, 'pz', split_axis=2, concat_axis=1, tiled=True)  102 us
    psum x1, blocking collectives, local(): numer, denom = lax.psum((local_lm, local_mm), ('px', 'pz'))  56.8 us
    all_to_all x1, starting transfers between devices, local(): lax.all_to_all(leonard, 'pz', split_axis=1, concat_axis=2, tiled=True)  25.5 us
    dot_general x1, matrix products, local(): jnp.einsum('ab,kbzx->kazx', weights, smooth_boxed, precision=lax.Precisio...  8.81 us
    all_to_all x1, starting transfers between devices, local(): lax.all_to_all(boxed, 'pz', split_axis=2, concat_axis=1, tiled=True)  7.84 us
    ppermute x2, starting transfers between devices, with_halo(): lax.ppermute(tail, axis, [(i, (i + 1) % count) for i in range(ends)])  5.12 us
  transfers between devices with their start and end apart: 6, of which 4 were waited for; matrix products, arithmetic and copies ran while one was open for 1% of the time, Pallas kernels for 0%

commit v1 on v0

--- a/solution.py
+++ b/solution.py
@@ -103,7 +103,10 @@
     cells = filtered.shape[3] * lax.axis_size("px") * filtered.shape[2] * lax.axis_size("pz")
     per_bin = numer / jnp.maximum(denom, jnp.float32(cells))
     coefficient = jnp.dot(onehot, per_bin, precision=lax.Precision.HIGHEST)
-    leonard_back = lax.all_to_all(leonard, "pz", split_axis=1, concat_axis=2, tiled=True)
+    leonard_back = jnp.concatenate(
+        lax.all_to_all(jnp.stack(jnp.split(leonard, lax.axis_size("pz"), axis=1)), "pz", 0, 0),
+        axis=2,
+    )
     offset = lax.axis_index("pz") * local_planes
     local_coef = lax.dynamic_slice_in_dim(coefficient, offset, local_planes, 0)
     viscosity = local_coef[:, None, None] * magnitude

time: 247 us -> 289 us (1.17)
  local copies, waits for them, and re-layouts: 14 us -> 54.6 us
    another operation x0 -> x18, local copies, waits for them, and re-layouts: none -> 31.9 us  [local(): jnp.stack(jnp.split(leonard, lax.axis_size('pz'), axis=1))]
    unnamed x21 -> x52, local copies, waits for them, and re-layouts: 4.01 us -> 16 us
where the time goes in v1:
time: 289 us; the launch traced here: 288 us
  waiting for transfers between devices  107 us (37%)
  blocking collectives  56.8 us (20%)
  local copies, waits for them, and re-layouts  54.6 us (19%)
  starting transfers between devices  40.2 us (14%)
  other arithmetic  18.2 us (6%)
  matrix products  9.47 us (3%)
    all_to_all x1, waiting for transfers between devices, local(): lax.all_to_all(boxed, 'pz', split_axis=2, concat_axis=1, tiled=True)  102 us
    psum x1, blocking collectives, local(): numer, denom = lax.psum((local_lm, local_mm), ('px', 'pz'))  56.8 us
    another operation x18, local copies, waits for them, and re-layouts, local(): jnp.stack(jnp.split(leonard, lax.axis_size('pz'), axis=1))  31.9 us
    all_to_all x1, starting transfers between devices, local(): lax.all_to_all(jnp.stack(jnp.split(leonard, lax.axis_size('pz'), axis=1))...  25.5 us
    unnamed x52, local copies, waits for them, and re-layouts  16 us
    dot_general x1, matrix products, local(): jnp.einsum('ab,kbzx->kazx', weights, smooth_boxed, precision=lax.Precisio...  8.81 us
    all_to_all x1, starting transfers between devices, local(): lax.all_to_all(boxed, 'pz', split_axis=2, concat_axis=1, tiled=True)  8.05 us
  transfers between devices with their start and end apart: 6, of which 4 were waited for; matrix products, arithmetic and copies ran while one was open for 1% of the time, Pallas kernels for 0%

profile of v1, /device:TPU:0, one launch (start us, length us, event | category | flops | bytes accessed | tf_op | source)
XLA Modules:
  0.0 287.6 jit_solution(6737788298393811100)
XLA Ops:
  0.6 1.7 fusion.38
  6.0 4.6 %collective-permute-start.2 = (f32[3,1,32,132]{3,1,0,2:T(1,128)S(1)}, f32[3,1,32,132]{3,1,0,2:T(1,128)S(1)}, u32[]{:S(2)}, u32[]{:S(2)}) collective-permute-start(f32[3,1,32,132]{3,1,0,2:T(1,128)S(1)} %get-tuple-element.30), channel_id=1, source_target_pairs={{0,1},{1,2},{2,3},{3,4},{4,5},{5,6},{6,7},{7,8},{8,9},{9,10},{10,1... | collective-permute-start | bytes 152072 | tf_op jit(solution)/shard_map/ppermute | solution.py:17
  10.6 1.5 collective-permute-start.3
  13.1 4.1 %collective-permute-done.3 = f32[3,1,32,132]{3,1,0,2:T(1,128)S(1)} collective-permute-done((f32[3,1,32,132]{3,1,0,2:T(1,128)S(1)}, f32[3,1,32,132]{3,1,0,2:T(1,128)S(1)}, u32[]{:S(2)}, u32[]{:S(2)}) %collective-permute-start.3) | collective-permute-done | bytes 50720 | tf_op jit(solution)/shard_map/ppermute | solution.py:19
  17.4 1.0 pad_maximum_fusion
  18.5 3.0 %fusion.6 = (f32[3,16,34,130]{3,1,0,2:T(8,128)}, f32[3,16,34,130]{3,1,0,2:T(8,128)S(1)}, f32[21,16,34,130]{3,1,0,2:T(8,128)S(1)}) fusion(f32[3,18,36,132]{3,1,0,2:T(8,128)S(1)} %pad_maximum_fusion), kind=kLoop, calls=%fused_computation.25 | loop fusion | flops 848639 | bytes 8434176 | tf_op jit(solution)/shard_map/mul | solution.py:28
  21.6 1.3 copy-done.1
  23.1 2.1 fusion.5
  28.9 3.2 %fusion = f32[21,16,34,128]{3,1,0,2:T(8,128)S(1)} fusion(f32[21,16,34,130]{3,1,0,2:T(8,128)S(1)} %multiply_dynamic-update-slice_fusion), kind=kLoop, calls=%fused_computation.1 | loop fusion | flops 5849088 | bytes 23396352 | tf_op jit(solution)/shard_map/mul | solution.py:56
  32.1 3.1 %fusion.2 = f32[21,16,32,128]{3,1,0,2:T(8,128)} fusion(f32[21,16,34,128]{3,1,0,2:T(8,128)S(1)} %fusion), kind=kLoop, calls=%fused_computation.5 | loop fusion | flops 5505024 | bytes 22020096 | tf_op jit(solution)/shard_map/mul | solution.py:57
  35.2 8.0 %all-to-all-start = ((f32[21,16,32,128]{3,1,0,2:T(8,128)}), f32[21,16,32,128]{3,1,0,2:T(8,128)}, u32[]{:S(2)}, u32[]{:S(2)}) async-start(f32[21,16,32,128]{3,1,0,2:T(8,128)} %fusion.2), calls=%async_computation | async-start | bytes 11010048 | tf_op jit(solution)/shard_map/all_to_all | solution.py:96
  43.5 101.8 %all-to-all-done = f32[21,16,32,128]{3,1,0,2:T(8,128)} async-done(((f32[21,16,32,128]{3,1,0,2:T(8,128)}), f32[21,16,32,128]{3,1,0,2:T(8,128)}, u32[]{:S(2)}, u32[]{:S(2)}) %all-to-all-start) | async-done | bytes 5505056 | tf_op jit(solution)/shard_map/all_to_all | solution.py:96
  145.3 3.3 %copy.28 = f32[21,16,16,2,128]{4,2,1,3,0:T(8,128)S(1)} copy(f32[21,16,16,2,128]{4,2,0,3,1:T(8,128)} %bitcast.2) | data formatting | bytes 11010048 | tf_op jit(solution)/shard_map/all_to_all | solution.py:96
  148.6 8.8 %convolution_bitcast_fusion = f32[21,256,2,128]{1,3,2,0:T(8,128)S(1)} fusion(f32[21,256,2,128]{3,1,2,0:T(8,128)S(1)} %bitcast.59, f32[256,256]{1,0:T(8,128)S(1)} %copy-done.2, f32[256]{0:T(256)S(1)} %fusion.19, s32[256]{0:T(256)S(1)} %copy-done.11), kind=kOutput, calls=%fused_computation.10 | convolution fusion | flops 4228055040 | bytes 11274240 | tf_op jit(solution)/shard_map/ab,kbzx->kazx/dot_general | solution.py:97
  159.1 7.0 %slice_bitcast_fusion = (f32[1,6,16,2,128]{2,4,3,1,0:T(8,128)}, f32[1,6,16,2,128]{2,4,3,1,0:T(8,128)}, f32[1,6,16,2,128]{2,4,3,1,0:T(8,128)}, f32[1,6,16,2,128]{...) fusion(f32[6,256,2,128]{1,3,2,0:T(8,128)S(1)} %get-tuple-element.18), kind=kLoop, calls=%fused_computation.44 | loop fusion | bytes 3145728 | tf_op jit(solution)/shard_map/stack | solution.py:107
  166.1 1.4 copy.45
  167.5 1.4 copy.44
  168.9 1.4 copy.43
  170.2 1.4 copy.42
  171.6 1.4 copy.41
  173.0 1.4 copy.40
  174.3 2.0 copy.39
  176.4 2.0 copy.38
  178.4 2.0 copy.37
  180.4 2.0 copy.36
  182.4 2.0 copy.35
  184.4 2.0 copy.34
  186.4 2.0 copy.33
  191.1 1.5 constant_dynamic-update-slice_fusion.26
  201.7 25.5 %all-to-all-start.1 = ((f32[16,6,16,2,128]{4,2,3,1,0:T(8,128)}), f32[16,6,16,2,128]{4,2,3,1,0:T(8,128)S(1)}, u32[]{:S(2)}, u32[]{:S(2)}) async-start(f32[16,6,16,2,128]{4,2,3,1,0:T(8,128)} %constant_dynamic-update-slice_fusion.12), calls=%async_computation.1 | async-start | bytes 3145728 | tf_op jit(solution)/shard_map/all_to_all | solution.py:107
  227.7 56.8 %all-reduce = (f32[64]{0:T(128)S(1)}, f32[64]{0:T(128)S(1)}) all-reduce(f32[64]{0:T(128)S(1)} %convolution_bitcast_fusion.2, f32[64]{0:T(128)S(1)} %convolution_bitcast_fusion.1), channel_id=1, replica_groups=mesh['px'=2,'pz'=16] {'px','pz'}, use_global_device_ids=true, to_apply=%region_6.0 | all-reduce | flops 128 | bytes 1024 | tf_op jit(solution)/shard_map/psum | solution.py:102
  286.0 1.6 copy.47
  (95 shorter events, 24.1 us)
Async XLA Ops:
  0.6 3.1 %copy-start = (f32[3,16,32,128]{3,2,1,0:T(8,128)S(1)}, f32[3,16,32,128]{3,2,1,0:T(8,128)}, u32[]{:S(2)}) copy-start(f32[3,16,32,128]{3,2,1,0:T(8,128)} %param.5) | copy-start | bytes 2359300
  2.7 1.4 collective-permute-start
  3.6 1.3 collective-permute-start.1
  6.0 7.1 %collective-permute-start.2 = (f32[3,1,32,132]{3,1,0,2:T(1,128)S(1)}, f32[3,1,32,132]{3,1,0,2:T(1,128)S(1)}, u32[]{:S(2)}, u32[]{:S(2)}) collective-permute-start(f32[3,1,32,132]{3,1,0,2:T(1,128)S(1)} %get-tuple-element.30), channel_id=1, source_target_pairs={{0,1},{1,2},{2,3},{3,4},{4,5},{5,6},{6,7},{7,8},{8,9},{9,10},{10,1... | collective-permute-start | bytes 152072 | tf_op jit(solution)/shard_map/ppermute | solution.py:17
  10.6 6.6 %collective-permute-start.3 = (f32[3,1,32,132]{3,1,0,2:T(1,128)S(1)}, f32[3,1,32,132]{3,1,0,2:T(1,128)S(1)}, u32[]{:S(2)}, u32[]{:S(2)}) collective-permute-start(f32[3,1,32,132]{3,1,0,2:T(1,128)S(1)} %get-tuple-element.31), channel_id=1, source_target_pairs={{1,0},{2,1},{3,2},{4,3},{5,4},{6,5},{7,6},{8,7},{9,8},{10,9},{11,1... | collective-permute-start | bytes 152072 | tf_op jit(solution)/shard_map/ppermute | solution.py:19
  21.5 1.4 copy-start.1
  35.2 8.1 %copy-start.2 = (f32[256,256]{1,0:T(8,128)S(1)}, f32[256,256]{1,0:T(8,128)}, u32[]{:S(2)}) copy-start(f32[256,256]{1,0:T(8,128)} %param.6) | copy-start | bytes 786436
  35.2 8.1 %copy-start.11 = (s32[256]{0:T(256)S(1)}, s32[256]{0:T(256)}, u32[]{:S(2)}) copy-start(s32[256]{0:T(256)} %param.7) | copy-start | bytes 3076
  35.2 110.0 %all-to-all-start = ((f32[21,16,32,128]{3,1,0,2:T(8,128)}), f32[21,16,32,128]{3,1,0,2:T(8,128)}, u32[]{:S(2)}, u32[]{:S(2)}) async-start(f32[21,16,32,128]{3,1,0,2:T(8,128)} %fusion.2), calls=%async_computation | async-start | bytes 11010048 | tf_op jit(solution)/shard_map/all_to_all | solution.py:96
  157.6 0.7 copy-start.12
  189.3 3.4 %copy-start.10 = (f32[1,6,16,2,128]{4,2,3,1,0:T(8,128)S(1)}, f32[1,6,16,2,128]{4,2,3,1,0:T(8,128)}, u32[]{:S(2)}) copy-start(f32[1,6,16,2,128]{4,2,3,1,0:T(8,128)} %copy.32) | copy-start | bytes 294916
  189.3 4.0 %copy-start.9 = (f32[1,6,16,2,128]{4,2,3,1,0:T(8,128)S(1)}, f32[1,6,16,2,128]{4,2,3,1,0:T(8,128)}, u32[]{:S(2)}) copy-start(f32[1,6,16,2,128]{4,2,3,1,0:T(8,128)} %copy.33) | copy-start | bytes 294916
  189.3 4.7 %copy-start.8 = (f32[1,6,16,2,128]{4,2,3,1,0:T(8,128)S(1)}, f32[1,6,16,2,128]{4,2,3,1,0:T(8,128)}, u32[]{:S(2)}) copy-start(f32[1,6,16,2,128]{4,2,3,1,0:T(8,128)} %copy.34) | copy-start | bytes 294916
  189.3 5.3 %copy-start.7 = (f32[1,6,16,2,128]{4,2,3,1,0:T(8,128)S(1)}, f32[1,6,16,2,128]{4,2,3,1,0:T(8,128)}, u32[]{:S(2)}) copy-start(f32[1,6,16,2,128]{4,2,3,1,0:T(8,128)} %copy.35) | copy-start | bytes 294916
  189.3 6.0 %copy-start.6 = (f32[1,6,16,2,128]{4,2,3,1,0:T(8,128)S(1)}, f32[1,6,16,2,128]{4,2,3,1,0:T(8,128)}, u32[]{:S(2)}) copy-start(f32[1,6,16,2,128]{4,2,3,1,0:T(8,128)} %copy.36) | copy-start | bytes 294916
  189.3 6.6 %copy-start.5 = (f32[1,6,16,2,128]{4,2,3,1,0:T(8,128)S(1)}, f32[1,6,16,2,128]{4,2,3,1,0:T(8,128)}, u32[]{:S(2)}) copy-start(f32[1,6,16,2,128]{4,2,3,1,0:T(8,128)} %copy.37) | copy-start | bytes 294916
  189.3 7.2 %copy-start.4 = (f32[1,6,16,2,128]{4,2,3,1,0:T(8,128)S(1)}, f32[1,6,16,2,128]{4,2,3,1,0:T(8,128)}, u32[]{:S(2)}) copy-start(f32[1,6,16,2,128]{4,2,3,1,0:T(8,128)} %copy.38) | copy-start | bytes 294916
  189.3 7.9 %copy-start.3 = (f32[1,6,16,2,128]{4,2,3,1,0:T(8,128)S(1)}, f32[1,6,16,2,128]{4,2,3,1,0:T(8,128)}, u32[]{:S(2)}) copy-start(f32[1,6,16,2,128]{4,2,3,1,0:T(8,128)} %copy.39) | copy-start | bytes 294916
  201.1 26.1 %copy-start.13 = (s32[256]{0:T(256)S(1)}, s32[256]{0:T(256)}, u32[]{:S(2)}) copy-start(s32[256]{0:T(256)} %param.8) | copy-start | bytes 3076
  201.7 84.1 %all-to-all-start.1 = ((f32[16,6,16,2,128]{4,2,3,1,0:T(8,128)}), f32[16,6,16,2,128]{4,2,3,1,0:T(8,128)S(1)}, u32[]{:S(2)}, u32[]{:S(2)}) async-start(f32[16,6,16,2,128]{4,2,3,1,0:T(8,128)} %constant_dynamic-update-slice_fusion.12), calls=%async_computation.1 | async-start | bytes 3145728 | tf_op jit(solution)/shard_map/all_to_all | solution.py:107
  284.7 1.2 copy-start.14
